TPU v7x, 32 devices: a whole 2x2x4 slice. The times are simulated.
32 devices in a mesh: dp: 2 (over core), expert: 16 (over z, y, x).
Axes of the slice: x: 2, y: 2, z: 4, core: 2. Of those that a mesh axis runs over, the one named last changes fastest.
Arguments:
- tokens: bfloat16 [8192, 1280], P(('dp', 'expert')), may hold values from -48 to 48
- phi: bfloat16 [1280, 48], replicated, may hold values from -0.05 to 0.05
- slot_count: int32 [16], replicated, may hold values from 1 to 3, 40 in all
- w_in: bfloat16 [16, 2560, 1280], P('expert'), may hold values from -1.25 to 1.25
- w_out: bfloat16 [16, 2560, 1280], P('expert'), may hold values from -1 to 1
- grad_out: bfloat16 [8192, 1280], P(('dp', 'expert')), may hold values from -6 to 6
Outputs:
- mixed_out: bfloat16 [8192, 1280], P(('dp', 'expert'))
- grad_tokens: bfloat16 [8192, 1280], P(('dp', 'expert'))
- grad_phi: float32 [1280, 48], replicated
- grad_w_in: bfloat16 [16, 2560, 1280], P('expert', 'dp')
- grad_w_out: bfloat16 [16, 2560, 1280], P('expert', 'dp')
Inputs may be any that keep to these rules, and one draw needn't show every extreme that they name: slot_count sums to 40; some expert has exactly 3.
All inputs are finite; a program needn't handle non-finite values.
Results may differ from a plain program's by a relative error of at most 0.012.
The roundings to bfloat16 on the way count: a program that leaves them out, or rounds other values in their place, can miss the bound.
Values may be sent and summed in bfloat16 or wider, within the bound.
A program may use at most 128 MiB of HBM per device.

v0:
```python
import jax
import jax.numpy as jnp
from jax import lax
from jax.sharding import PartitionSpec as P

D = 1280
MOST = 3


SQRT_HALF = 0.7071067811865476
INV_SQRT_TAU = 0.3989422804014327


def contract(left, right, left_dim, right_dim):
    return lax.dot_general(
        left, right, (((left_dim,), (right_dim,)), ((), ())), preferred_element_type=jnp.float32
    )


def softmax_along(logits, axis):
    maximum = jnp.max(logits, axis=axis, keepdims=True)
    weights = jnp.exp(logits - maximum)
    return weights / jnp.sum(weights, axis=axis, keepdims=True)


def gelu_parts(preact):
    normal_cdf = 0.5 * (1.0 + jax.scipy.special.erf(preact * SQRT_HALF))
    density = jnp.exp(-0.5 * preact * preact) * INV_SQRT_TAU
    return (preact * normal_cdf, normal_cdf + preact * density)


def live_slots(slot_count):
    positions = lax.broadcasted_iota(jnp.int32, (slot_count.shape[0], MOST), 1)
    return (positions < slot_count[:, None]).reshape(-1)


def image_front(image_tokens, phi, live_mask):
    logits = jnp.dot(image_tokens, phi, preferred_element_type=jnp.float32)
    spread = softmax_along(logits, 0)
    spread_b = spread.astype(jnp.bfloat16)
    slot_in = contract(spread_b, image_tokens, 0, 0).astype(jnp.bfloat16)
    mixing = softmax_along(jnp.where(live_mask[None, :], logits, -1e30), 1)
    return (slot_in, spread, spread_b, mixing)


def image_returned(
    image_tokens, phi, output_cotangent, slot_values, slot_grads, spread, spread_b, mixing
):
    d_mix = contract(output_cotangent, slot_values, 1, 1)
    d_comb = mixing * (d_mix - jnp.sum(d_mix * mixing, axis=1, keepdims=True))
    d_spread = contract(image_tokens, slot_grads, 1, 1)
    d_disp = spread * (d_spread - jnp.sum(d_spread * spread, axis=0, keepdims=True))
    d_logits = (d_comb + d_disp).astype(jnp.bfloat16)
    image_gradient = contract(d_logits, phi, 1, 1) + jnp.dot(
        spread_b, slot_grads, preferred_element_type=jnp.float32
    )
    return (image_gradient.astype(jnp.bfloat16), contract(image_tokens, d_logits, 0, 0))


def expert_front(slot_rows, first_proj, second_proj):
    preact = contract(slot_rows, first_proj, 1, 1)
    activated, slopes = gelu_parts(preact)
    hidden = activated.astype(jnp.bfloat16)
    return (jnp.dot(hidden, second_proj, preferred_element_type=jnp.float32), hidden, slopes)


def expert_back(slot_rows, hidden, slopes, row_grads, first_proj, second_proj):
    d_hidden = contract(row_grads, second_proj, 1, 1)
    grad_pre = (d_hidden * slopes).astype(jnp.bfloat16)
    grad_rows = jnp.dot(grad_pre, first_proj, preferred_element_type=jnp.float32)
    grad_first = contract(grad_pre, slot_rows, 0, 0)
    grad_second = contract(hidden, row_grads, 0, 0)
    return (grad_rows, grad_first, grad_second)


def local(tokens, phi, slot_count, w_in, w_out, grad_out):
    live_mask = live_slots(slot_count)
    experts = slot_count.shape[0]
    slot_in, spread, spread_b, mixing = image_front(tokens, phi, live_mask)
    mixing_b = mixing.astype(jnp.bfloat16)
    slot_cot = contract(mixing_b, grad_out, 0, 0).astype(jnp.bfloat16)
    outgoing = (slot_in.reshape(experts, MOST, D), slot_cot.reshape(experts, MOST, D))
    arrived_rows, arrived_grads = (
        lax.all_to_all(outgoing[0], "expert", split_axis=0, concat_axis=0, tiled=True),
        lax.all_to_all(outgoing[1], "expert", split_axis=0, concat_axis=0, tiled=True),
    )
    slot_rows = arrived_rows.reshape(-1, D)
    row_grads = arrived_grads.reshape(-1, D)
    first_proj = w_in[0]
    second_proj = w_out[0]
    half_width = first_proj.shape[0] // lax.axis_size("dp")
    offset = lax.axis_index("dp") * half_width
    first_half = lax.dynamic_slice_in_dim(first_proj, offset, half_width, 0)
    second_half = lax.dynamic_slice_in_dim(second_proj, offset, half_width, 0)
    both_rows, both_grads = (
        lax.all_gather(slot_rows, "dp", axis=0, tiled=True),
        lax.all_gather(row_grads, "dp", axis=0, tiled=True),
    )
    values, hidden, slopes = expert_front(both_rows, first_half, second_half)
    grad_rows, grad_first, grad_second = expert_back(
        both_rows, hidden, slopes, both_grads, first_half, second_half
    )
    values, grad_rows = (
        lax.psum_scatter(values, "dp", scatter_dimension=0, tiled=True),
        lax.psum_scatter(grad_rows, "dp", scatter_dimension=0, tiled=True),
    )
    returning = (
        values.astype(jnp.bfloat16).reshape(-1, MOST, D),
        grad_rows.astype(jnp.bfloat16).reshape(-1, MOST, D),
    )
    back_values, back_grads = (
        lax.all_to_all(returning[0], "expert", split_axis=0, concat_axis=0, tiled=True),
        lax.all_to_all(returning[1], "expert", split_axis=0, concat_axis=0, tiled=True),
    )
    slot_values = back_values.reshape(-1, D)
    slot_grads = back_grads.reshape(-1, D)
    mixed_out = jnp.dot(mixing_b, slot_values, preferred_element_type=jnp.float32).astype(
        jnp.bfloat16
    )
    grad_tokens, gradient_piece = image_returned(
        tokens, phi, grad_out, slot_values, slot_grads, spread, spread_b, mixing
    )
    grad_phi = lax.psum(gradient_piece, ("dp", "expert"))
    return (
        mixed_out,
        grad_tokens,
        grad_phi,
        grad_first.astype(jnp.bfloat16)[None],
        grad_second.astype(jnp.bfloat16)[None],
    )


def solution(mesh):
    placed = (
        P(("dp", "expert"), None),
        P(),
        P(),
        P("expert", None, None),
        P("expert", None, None),
        P(("dp", "expert"), None),
    )
    return jax.shard_map(
        local,
        mesh=mesh,
        in_specs=placed,
        out_specs=(
            P(("dp", "expert"), None),
            P(("dp", "expert"), None),
            P(),
            P("expert", "dp", None),
            P("expert", "dp", None),
        ),
        check_vma=False,
    )
```

profile of v0, /device:TPU:0, one launch (start us, length us, event | category | flops | bytes accessed | tf_op | source)
XLA Modules:
  0.0 219.8 jit_solution(17341292940598299620)
XLA Ops:
  8.3 1.4 select_reduce_fusion
  10.9 8.3 %all-to-all-start = ((bf16[16,3,1280]{2,1,0:T(4,128)(2,1)}), bf16[16,3,1280]{2,1,0:T(4,128)(2,1)S(1)}, u32[]{:S(2)}, u32[]{:S(2)}) async-start(bf16[16,3,1280]{2,1,0:T(4,128)(2,1)} %reshape.57), calls=%async_computation | async-start | bytes 327680 | tf_op jit(solution)/shard_map/all_to_all | solution.py:84
  19.2 1.4 convolution_convert_fusion.3
  21.3 5.8 %all-to-all-done = bf16[16,3,1280]{2,1,0:T(4,128)(2,1)S(1)} async-done(((bf16[16,3,1280]{2,1,0:T(4,128)(2,1)}), bf16[16,3,1280]{2,1,0:T(4,128)(2,1)S(1)}, u32[]{:S(2)}, u32[]{:S(2)}) %all-to-all-start) | async-done | bytes 122912 | tf_op jit(solution)/shard_map/all_to_all | solution.py:84
  27.1 3.5 %all-to-all-start.2 = ((bf16[16,3,1280]{2,1,0:T(4,128)(2,1)}), bf16[16,3,1280]{2,1,0:T(4,128)(2,1)S(1)}, u32[]{:S(2)}, u32[]{:S(2)}) async-start(bf16[16,3,1280]{2,1,0:T(4,128)(2,1)} %reshape.61), calls=%async_computation.3 | async-start | bytes 327680 | tf_op jit(solution)/shard_map/all_to_all | solution.py:85
  30.8 2.0 all_gather.6
  32.8 5.7 %all-to-all-done.2 = bf16[16,3,1280]{2,1,0:T(4,128)(2,1)S(1)} async-done(((bf16[16,3,1280]{2,1,0:T(4,128)(2,1)}), bf16[16,3,1280]{2,1,0:T(4,128)(2,1)S(1)}, u32[]{:S(2)}, u32[]{:S(2)}) %all-to-all-start.2) | async-done | bytes 122912 | tf_op jit(solution)/shard_map/all_to_all | solution.py:85
  38.7 2.0 all_gather.7
  40.7 3.1 %fusion.8 = f32[96,1280]{1,0:T(8,128)S(1)} fusion(bf16[96,1280]{1,0:T(8,128)(2,1)S(1)} %all_gather.6, bf16[1,2560,1280]{2,1,0:T(8,128)(2,1)} %param.9, s32[]{:T(128)S(6)} %select_n.9), kind=kOutput, calls=%fused_computation.10 | convolution fusion | flops 314572800 | bytes 4014084 | tf_op jit(solution)/shard_map/dot_general | solution.py:15
  43.7 3.1 %fusion.18 = bf16[96,1280]{1,0:T(8,128)(2,1)S(1)} fusion(bf16[96,1280]{1,0:T(8,128)(2,1)S(1)} %all_gather.7, bf16[1,2560,1280]{2,1,0:T(8,128)(2,1)} %param.10, s32[]{:T(128)S(6)} %select_n.9, f32[96,1280]{1,0:T(8,128)S(1)} %fusion.8), kind=kOutput, calls=%fused_computation.20 | convolution fusion | flops 315801600 | bytes 4259844 | tf_op jit(solution)/shard_map/dot_general | solution.py:15
  46.8 3.4 %fusion.6 = f32[96,1280]{1,0:T(8,128)} fusion(bf16[96,1280]{1,0:T(8,128)(2,1)S(1)} %fusion.18, bf16[1,2560,1280]{2,1,0:T(8,128)(2,1)} %param.9, s32[]{:T(128)S(6)} %select_n.9), kind=kOutput, calls=%fused_computation.8 | convolution fusion | flops 314572800 | bytes 4014084 | tf_op jit(solution)/shard_map/dot_general | solution.py:70
  50.2 3.4 %fusion.4 = f32[96,1280]{1,0:T(8,128)} fusion(bf16[1,2560,1280]{2,1,0:T(8,128)(2,1)} %param.10, s32[]{:T(128)S(6)} %select_n.9, f32[96,1280]{1,0:T(8,128)S(1)} %fusion.8), kind=kOutput, calls=%fused_computation.6 | convolution fusion | flops 315187200 | bytes 4259844 | tf_op jit(solution)/shard_map/dot_general | solution.py:64
  53.6 2.0 reduce-scatter.5.cloned.1.call-done
  57.3 6.7 %all-to-all-start.3 = ((bf16[16,3,1280]{2,1,0:T(4,128)(2,1)}), bf16[16,3,1280]{2,1,0:T(4,128)(2,1)S(1)}, u32[]{:S(2)}, u32[]{:S(2)}) async-start(bf16[16,3,1280]{2,1,0:T(4,128)(2,1)} %reshape.63), calls=%async_computation.5 | async-start | bytes 327680 | tf_op jit(solution)/shard_map/all_to_all | solution.py:113
  64.0 2.8 %fusion = bf16[1,1280,1280]{2,1,0:T(8,128)(2,1)} fusion(bf16[96,1280]{1,0:T(8,128)(2,1)S(1)} %fusion.18, bf16[96,1280]{1,0:T(8,128)(2,1)S(1)} %all_gather.6), kind=kOutput, calls=%fused_computation.2 | convolution fusion | flops 316211200 | bytes 3768320 | tf_op jit(solution)/shard_map/dot_general | solution.py:15
  66.8 2.8 %fusion.1 = bf16[1,1280,1280]{2,1,0:T(8,128)(2,1)} fusion(bf16[96,1280]{1,0:T(8,128)(2,1)S(1)} %all_gather.7, f32[96,1280]{1,0:T(8,128)S(1)} %fusion.8), kind=kOutput, calls=%fused_computation.3 | convolution fusion | flops 316825600 | bytes 4014080 | tf_op jit(solution)/shard_map/dot_general | solution.py:15
  71.3 1.1 all-to-all-done.3
  72.4 5.8 %all-to-all-start.1 = ((bf16[16,3,1280]{2,1,0:T(4,128)(2,1)}), bf16[16,3,1280]{2,1,0:T(4,128)(2,1)S(1)}, u32[]{:S(2)}, u32[]{:S(2)}) async-start(bf16[16,3,1280]{2,1,0:T(4,128)(2,1)} %reshape.59), calls=%async_computation.2 | async-start | bytes 327680 | tf_op jit(solution)/shard_map/all_to_all | solution.py:112
  78.6 7.5 %all-to-all-done.1 = bf16[16,3,1280]{2,1,0:T(4,128)(2,1)S(1)} async-done(((bf16[16,3,1280]{2,1,0:T(4,128)(2,1)}), bf16[16,3,1280]{2,1,0:T(4,128)(2,1)S(1)}, u32[]{:S(2)}, u32[]{:S(2)}) %all-to-all-start.1) | async-done | bytes 122912 | tf_op jit(solution)/shard_map/all_to_all | solution.py:112
  86.6 1.0 convolution_bitcast_fusion
  88.1 1.3 fusion.14
  89.4 1.3 convolution_convert_fusion.2
  90.6 121.0 %all-reduce.2.cloned.1.call-done = f32[1280,48]{0,1:T(8,128)} async-done(((f32[1280,48]{0,1:T(8,128)}), f32[1280,48]{0,1:T(8,128)}) %all-reduce.2.cloned.1.call-update) | async-done | bytes 245776 | tf_op jit(solution)/shard_map/psum | solution.py:123
  211.6 1.7 copy.12
  (30 shorter events, 8.2 us)
Async XLA Ops:
  7.2 1.1 copy-start
  10.9 16.3 %all-to-all-start = ((bf16[16,3,1280]{2,1,0:T(4,128)(2,1)}), bf16[16,3,1280]{2,1,0:T(4,128)(2,1)S(1)}, u32[]{:S(2)}, u32[]{:S(2)}) async-start(bf16[16,3,1280]{2,1,0:T(4,128)(2,1)} %reshape.57), calls=%async_computation | async-start | bytes 327680 | tf_op jit(solution)/shard_map/all_to_all | solution.py:84
  27.1 11.4 %all-to-all-start.2 = ((bf16[16,3,1280]{2,1,0:T(4,128)(2,1)}), bf16[16,3,1280]{2,1,0:T(4,128)(2,1)S(1)}, u32[]{:S(2)}, u32[]{:S(2)}) async-start(bf16[16,3,1280]{2,1,0:T(4,128)(2,1)} %reshape.61), calls=%async_computation.3 | async-start | bytes 327680 | tf_op jit(solution)/shard_map/all_to_all | solution.py:85
  30.7 24.9 %reduce-scatter.5.cloned.1.call-start = ((), (), s32[]{:S(2)}) async-start(), calls=%async_computation.7 | async-start | bytes 737280 | tf_op jit(solution)/shard_map/reduce_scatter | solution.py:105
  50.2 19.4 %reduce-scatter.3.cloned.1.call-start = ((), (), s32[]{:S(2)}) async-start(), calls=%async_computation.6 | async-start | bytes 737280 | tf_op jit(solution)/shard_map/reduce_scatter | solution.py:104
  57.3 15.1 %all-to-all-start.3 = ((bf16[16,3,1280]{2,1,0:T(4,128)(2,1)}), bf16[16,3,1280]{2,1,0:T(4,128)(2,1)S(1)}, u32[]{:S(2)}, u32[]{:S(2)}) async-start(bf16[16,3,1280]{2,1,0:T(4,128)(2,1)} %reshape.63), calls=%async_computation.5 | async-start | bytes 327680 | tf_op jit(solution)/shard_map/all_to_all | solution.py:113
  66.8 19.4 %copy-start.1 = (bf16[256,1280]{1,0:T(8,128)(2,1)S(1)}, bf16[256,1280]{1,0:T(8,128)(2,1)}, u32[]{:S(2)}) copy-start(bf16[256,1280]{1,0:T(8,128)(2,1)} %param.11) | copy-start | bytes 1966084
  66.8 20.8 %copy-start.2 = (bf16[1280,48]{0,1:T(8,128)(2,1)S(1)}, bf16[1280,48]{0,1:T(8,128)(2,1)}, u32[]{:S(2)}) copy-start(bf16[1280,48]{0,1:T(8,128)(2,1)} %param.7) | copy-start | bytes 368644
  72.4 13.7 %all-to-all-start.1 = ((bf16[16,3,1280]{2,1,0:T(4,128)(2,1)}), bf16[16,3,1280]{2,1,0:T(4,128)(2,1)S(1)}, u32[]{:S(2)}, u32[]{:S(2)}) async-start(bf16[16,3,1280]{2,1,0:T(4,128)(2,1)} %reshape.59), calls=%async_computation.2 | async-start | bytes 327680 | tf_op jit(solution)/shard_map/all_to_all | solution.py:112
  78.2 133.4 %all-reduce.2.cloned.1.call-start = ((), (), s32[]{:S(2)}) async-start(), calls=%async_computation.8 | async-start | bytes 491520 | tf_op jit(solution)/shard_map/psum | solution.py:123
Sparse Core Ops, SparseCore 0:
  50.3 5.2 reduce-scatter.4
  58.5 9.0 reduce-scatter.2
  88.2 123.3 all-reduce.1
where the time goes:
time: 221 us; the launch traced here: 220 us
  waiting for transfers between devices  143 us (65%)
  matrix products  26 us (12%)
  starting transfers between devices  24.5 us (11%)
  between operations  13.9 us (6%)
  local copies, waits for them, and re-layouts  5.35 us (2%)
  blocking collectives  3.96 us (2%)
  other arithmetic  2.91 us (1%)
    psum x1, waiting for transfers between devices, local(): grad_phi = lax.psum(gradient_piece, ('dp', 'expert'))  121 us
    dot_general x10, matrix products, contract(): lax.dot_general(left, right, (((left_dim,), (right_dim,)), ((), ())), pre...  15.4 us
    all_to_all x1, starting transfers between devices, local(): lax.all_to_all(outgoing[0], 'expert', split_axis=0, concat_axis=0, tiled=...  8.34 us
    all_to_all x1, waiting for transfers between devices, local(): lax.all_to_all(returning[0], 'expert', split_axis=0, concat_axis=0, tiled...  7.48 us
    all_to_all x1, starting transfers between devices, local(): lax.all_to_all(returning[1], 'expert', split_axis=0, concat_axis=0, tiled...  6.74 us
    all_to_all x1, waiting for transfers between devices, local(): lax.all_to_all(outgoing[0], 'expert', split_axis=0, concat_axis=0, tiled=...  5.82 us
    all_to_all x1, starting transfers between devices, local(): lax.all_to_all(returning[0], 'expert', split_axis=0, concat_axis=0, tiled...  5.8 us
    all_to_all x1, waiting for transfers between devices, local(): lax.all_to_all(outgoing[1], 'expert', split_axis=0, concat_axis=0, tiled=...  5.75 us
  transfers between devices with their start and end apart: 7, of which 6 were waited for; matrix products, arithmetic and copies ran while one was open for 8% of the time, Pallas kernels for 0%

commit v1 on v0

--- a/solution.py
+++ b/solution.py
@@ -54,7 +54,7 @@
     image_gradient = contract(d_logits, phi, 1, 1) + jnp.dot(
         spread_b, slot_grads, preferred_element_type=jnp.float32
     )
-    return (image_gradient.astype(jnp.bfloat16), contract(image_tokens, d_logits, 0, 0))
+    return (image_gradient.astype(jnp.bfloat16), contract(d_logits, image_tokens, 0, 0))
 
 
 def expert_front(slot_rows, first_proj, second_proj):
@@ -73,54 +73,70 @@
     return (grad_rows, grad_first, grad_second)
 
 
+def sum_own_half(partial):
+    rows = partial.shape[0] // 2
+    mine = lax.axis_index("dp")
+    kept = lax.dynamic_slice_in_dim(partial, mine * rows, rows, 0)
+    given = lax.dynamic_slice_in_dim(partial, (1 - mine) * rows, rows, 0)
+    return kept + lax.ppermute(given, "dp", [(0, 1), (1, 0)])
+
+
+def sum_everywhere(term, experts):
+    swap = [(0, 1), (1, 0)]
+    half = D // 2
+    mine = lax.axis_index("dp")
+    kept = lax.dynamic_slice_in_dim(term, mine * half, half, 1)
+    given = lax.dynamic_slice_in_dim(term, (1 - mine) * half, half, 1)
+    term = kept + lax.ppermute(given, "dp", swap)
+    pieces = lax.all_to_all(
+        term.reshape(experts, -1, 128), "expert", split_axis=0, concat_axis=0, tiled=True
+    )
+    piece = jnp.sum(pieces, axis=0)
+    copies = jnp.broadcast_to(piece[None], (experts,) + piece.shape)
+    whole = lax.all_to_all(copies, "expert", split_axis=0, concat_axis=0, tiled=True)
+    whole = whole.reshape(-1, half)
+    other = lax.ppermute(whole, "dp", swap)
+    first = jnp.where(mine == 0, whole, other)
+    second = jnp.where(mine == 0, other, whole)
+    return jnp.concatenate([first, second], axis=1).T
+
+
 def local(tokens, phi, slot_count, w_in, w_out, grad_out):
     live_mask = live_slots(slot_count)
     experts = slot_count.shape[0]
     slot_in, spread, spread_b, mixing = image_front(tokens, phi, live_mask)
     mixing_b = mixing.astype(jnp.bfloat16)
     slot_cot = contract(mixing_b, grad_out, 0, 0).astype(jnp.bfloat16)
-    outgoing = (slot_in.reshape(experts, MOST, D), slot_cot.reshape(experts, MOST, D))
-    arrived_rows, arrived_grads = (
-        lax.all_to_all(outgoing[0], "expert", split_axis=0, concat_axis=0, tiled=True),
-        lax.all_to_all(outgoing[1], "expert", split_axis=0, concat_axis=0, tiled=True),
-    )
-    slot_rows = arrived_rows.reshape(-1, D)
-    row_grads = arrived_grads.reshape(-1, D)
+    outgoing = jnp.concatenate([slot_in, slot_cot], axis=1).reshape(experts, -1, 128)
+    arrived = lax.all_to_all(outgoing, "expert", split_axis=0, concat_axis=0, tiled=True)
+    arrived = arrived.reshape(-1, 2 * D)
     first_proj = w_in[0]
     second_proj = w_out[0]
     half_width = first_proj.shape[0] // lax.axis_size("dp")
     offset = lax.axis_index("dp") * half_width
     first_half = lax.dynamic_slice_in_dim(first_proj, offset, half_width, 0)
     second_half = lax.dynamic_slice_in_dim(second_proj, offset, half_width, 0)
-    both_rows, both_grads = (
-        lax.all_gather(slot_rows, "dp", axis=0, tiled=True),
-        lax.all_gather(row_grads, "dp", axis=0, tiled=True),
-    )
+    both = lax.all_gather(arrived, "dp", axis=0, tiled=True)
+    both_rows, both_grads = both[:, :D], both[:, D:]
     values, hidden, slopes = expert_front(both_rows, first_half, second_half)
     grad_rows, grad_first, grad_second = expert_back(
         both_rows, hidden, slopes, both_grads, first_half, second_half
     )
-    values, grad_rows = (
-        lax.psum_scatter(values, "dp", scatter_dimension=0, tiled=True),
-        lax.psum_scatter(grad_rows, "dp", scatter_dimension=0, tiled=True),
-    )
-    returning = (
-        values.astype(jnp.bfloat16).reshape(-1, MOST, D),
-        grad_rows.astype(jnp.bfloat16).reshape(-1, MOST, D),
-    )
-    back_values, back_grads = (
-        lax.all_to_all(returning[0], "expert", split_axis=0, concat_axis=0, tiled=True),
-        lax.all_to_all(returning[1], "expert", split_axis=0, concat_axis=0, tiled=True),
-    )
-    slot_values = back_values.reshape(-1, D)
-    slot_grads = back_grads.reshape(-1, D)
+    values = sum_own_half(values)
+    grad_rows = sum_own_half(grad_rows)
+    returning = jnp.concatenate(
+        [values.astype(jnp.bfloat16), grad_rows.astype(jnp.bfloat16)], axis=1
+    ).reshape(lax.axis_size("expert"), -1, 128)
+    back = lax.all_to_all(returning, "expert", split_axis=0, concat_axis=0, tiled=True)
+    back = back.reshape(-1, 2 * D)
+    slot_values, slot_grads = back[:, :D], back[:, D:]
     mixed_out = jnp.dot(mixing_b, slot_values, preferred_element_type=jnp.float32).astype(
         jnp.bfloat16
     )
     grad_tokens, gradient_piece = image_returned(
         tokens, phi, grad_out, slot_values, slot_grads, spread, spread_b, mixing
     )
-    grad_phi = lax.psum(gradient_piece, ("dp", "expert"))
+    grad_phi = sum_everywhere(gradient_piece, experts)
     return (
         mixed_out,
         grad_tokens,
@@ -139,6 +155,7 @@
         P("expert", None, None),
         P(("dp", "expert"), None),
     )
+
     return jax.shard_map(
         local,
         mesh=mesh,

time: 221 us -> 85 us (0.38)
  waiting for transfers between devices: 143 us -> 33.2 us
  between operations: 13.9 us -> 0.86 us
  starting transfers between devices: 24.5 us -> 19.7 us
  matrix products: 26 us -> 22.2 us
    psum x1 -> x0, waiting for transfers between devices: 121 us -> none  [local(): grad_phi = lax.psum(gradient_piece, ('dp', 'expert'))]
    all_to_all x4, waiting for transfers between devices: 20.2 us -> 32 us  [the longest x1 9.86 us: local(): lax.all_to_all(outgoing, 'expert', split_axis=0, concat_axis=0, tiled=True)]
    all_to_all x4, starting transfers between devices: 24.4 us -> 18.9 us  [the longest x1 8.34 us: local(): lax.all_to_all(outgoing, 'expert', split_axis=0, concat_axis=0, tiled=True)]
    dot_general x1, matrix products: 3.38 us -> 0.67 us  [expert_back(): jnp.dot(grad_pre, first_proj, preferred_element_type=jnp.float32)]
  transfers between devices with their start and end apart: 7 -> 8, of which waited for: 6 -> 6; matrix products, arithmetic and copies ran while one was open for 8% -> 11% of each run, Pallas kernels for 0% -> 0%
where the time goes in v1:
time: 85 us; the launch traced here: 84.4 us
  waiting for transfers between devices  33.2 us (39%)
  matrix products  22.2 us (26%)
  starting transfers between devices  19.7 us (23%)
  local copies, waits for them, and re-layouts  4.46 us (5%)
  blocking collectives  2.16 us (3%)
  other arithmetic  1.87 us (2%)
  between operations  0.86 us (1%)
    dot_general x10, matrix products, contract(): lax.dot_general(left, right, (((left_dim,), (right_dim,)), ((), ())), pre...  14.8 us
    all_to_all x1, waiting for transfers between devices, local(): lax.all_to_all(outgoing, 'expert', split_axis=0, concat_axis=0, tiled=True)  9.86 us
    all_to_all x1, starting transfers between devices, local(): lax.all_to_all(outgoing, 'expert', split_axis=0, concat_axis=0, tiled=True)  8.34 us
    all_to_all x1, waiting for transfers between devices, sum_everywhere(): lax.all_to_all(term.reshape(experts, -1, 128), 'expert', split_axis=0, co...  7.85 us
    all_to_all x1, waiting for transfers between devices, local(): lax.all_to_all(returning, 'expert', split_axis=0, concat_axis=0, tiled=True)  7.84 us
    all_to_all x1, waiting for transfers between devices, sum_everywhere(): lax.all_to_all(copies, 'expert', split_axis=0, concat_axis=0, tiled=True)  6.49 us
    all_to_all x1, starting transfers between devices, local(): lax.all_to_all(returning, 'expert', split_axis=0, concat_axis=0, tiled=True)  3.55 us
    all_to_all x1, starting transfers between devices, sum_everywhere(): lax.all_to_all(term.reshape(experts, -1, 128), 'expert', split_axis=0, co...  3.52 us
  transfers between devices with their start and end apart: 8, of which 6 were waited for; matrix products, arithmetic and copies ran while one was open for 11% of the time, Pallas kernels for 0%

profile of v1, /device:TPU:0, one launch (start us, length us, event | category | flops | bytes accessed | tf_op | source)
XLA Modules:
  0.0 84.4 jit_solution(9365672044417261307)
XLA Ops:
  0.6 0.8 iota_compare_fusion
  1.7 1.4 %fusion.51 = (f32[48]{0:T(128)S(1)}, f32[256]{0:T(256)S(1)}, f32[256,48]{0,1:T(8,128)S(1)}) fusion(pred[48]{0:T(512)(128)(4,1)S(1)} %lt.35, bf16[256,1280]{1,0:T(8,128)(2,1)S(1)} %copy-done, bf16[1280,48]{0,1:T(8,128)(2,1)} %param.7), kind=kOutput, calls=%fused_computation.72 | convolution fusion | flops 31493840 | bytes 828656 | tf_op jit(solution)/shard_map/dot_general | solution.py:38
  3.6 1.4 %convolution_convert_fusion.3 = bf16[48,1280]{1,0:T(8,128)(2,1)S(1)} fusion(bf16[256,1280]{1,0:T(8,128)(2,1)} %param.11, f32[256,48]{0,1:T(8,128)S(1)} %get-tuple-element.13, f32[256]{0:T(256)S(1)} %get-tuple-element.8, f32[256]{0:T(256)S(1)} %get-tuple-element.10, pred[48]{0:T(512)(128)(4,1)S(1)} %lt.35), kind=kOutput, calls=%fused_computation.21 | convolution fusion | flops 31567872 | bytes 829488 | tf_op jit(solution)/shard_map/dot_general | solution.py:15
  5.0 1.0 %reshape.52 = bf16[16,60,128]{2,1,0:T(8,128)(2,1)} reshape(bf16[48,2560]{1,0:T(8,128)(2,1)S(1)} %pad_maximum_fusion) | data formatting | bytes 491520 | tf_op jit(solution)/shard_map/reshape | solution.py:110
  6.0 8.3 %all-to-all-start = ((bf16[16,60,128]{2,1,0:T(8,128)(2,1)}), bf16[16,60,128]{2,1,0:T(8,128)(2,1)S(1)}, u32[]{:S(2)}, u32[]{:S(2)}) async-start(bf16[16,60,128]{2,1,0:T(8,128)(2,1)} %reshape.52), calls=%async_computation | async-start | bytes 524288 | tf_op jit(solution)/shard_map/all_to_all | solution.py:111
  14.4 9.9 %all-to-all-done = bf16[16,60,128]{2,1,0:T(8,128)(2,1)S(1)} async-done(((bf16[16,60,128]{2,1,0:T(8,128)(2,1)}), bf16[16,60,128]{2,1,0:T(8,128)(2,1)S(1)}, u32[]{:S(2)}, u32[]{:S(2)}) %all-to-all-start) | async-done | bytes 245792 | tf_op jit(solution)/shard_map/all_to_all | solution.py:111
  24.5 2.2 %all_gather.3 = bf16[96,2560]{1,0:T(8,128)(2,1)S(1)} all-gather(bf16[48,2560]{1,0:T(8,128)(2,1)S(1)} %reshape.53), channel_id=1, replica_groups=mesh['dp'=2,'expert'=16] {'dp'}, dimensions={0}, use_global_device_ids=true | all-gather | bytes 737280 | tf_op jit(solution)/shard_map/all_gather | solution.py:119
  26.7 3.2 %fusion.8 = f32[96,1280]{1,0:T(8,128)S(1)} fusion(bf16[1,2560,1280]{2,1,0:T(8,128)(2,1)} %param.9, s32[]{:T(128)S(6)} %select_n.35, bf16[96,2560]{1,0:T(8,128)(2,1)S(1)} %all_gather.3), kind=kOutput, calls=%fused_computation.10 | convolution fusion | flops 314572800 | bytes 4014084 | tf_op jit(solution)/shard_map/dot_general | solution.py:15
  29.9 2.7 %fusion.4 = f32[96,1280]{1,0:T(8,128)S(1)} fusion(bf16[1,2560,1280]{2,1,0:T(8,128)(2,1)} %param.10, s32[]{:T(128)S(6)} %select_n.35, f32[96,1280]{1,0:T(8,128)S(1)} %fusion.8), kind=kOutput, calls=%fused_computation.6 | convolution fusion | flops 315187200 | bytes 4259844 | tf_op jit(solution)/shard_map/dot_general | solution.py:64
  32.7 3.1 %fusion.18 = bf16[96,1280]{1,0:T(8,128)(2,1)S(1)} fusion(bf16[1,2560,1280]{2,1,0:T(8,128)(2,1)} %param.10, s32[]{:T(128)S(6)} %select_n.35, f32[96,1280]{1,0:T(8,128)S(1)} %fusion.8, bf16[96,2560]{1,0:T(8,128)(2,1)S(1)} %all_gather.3), kind=kOutput, calls=%fused_computation.20 | convolution fusion | flops 315801600 | bytes 4259844 | tf_op jit(solution)/shard_map/dot_general | solution.py:15
  37.4 0.9 %collective-permute-done.1 = f32[48,1280]{1,0:T(8,128)S(1)} collective-permute-done((f32[48,1280]{1,0:T(8,128)S(1)}, f32[48,1280]{1,0:T(8,128)S(1)}, u32[]{:S(2)}, u32[]{:S(2)}) %collective-permute-start.1) | collective-permute-done | bytes 245792 | tf_op jit(solution)/shard_map/ppermute | solution.py:81
  38.4 1.0 %reshape.54 = bf16[16,60,128]{2,1,0:T(8,128)(2,1)} reshape(bf16[48,2560]{1,0:T(8,128)(2,1)S(1)} %pad_maximum_fusion.1) | data formatting | bytes 491520 | tf_op jit(solution)/shard_map/reshape | solution.py:129
  39.4 3.5 %all-to-all-start.1 = ((bf16[16,60,128]{2,1,0:T(8,128)(2,1)}), bf16[16,60,128]{2,1,0:T(8,128)(2,1)S(1)}, u32[]{:S(2)}, u32[]{:S(2)}) async-start(bf16[16,60,128]{2,1,0:T(8,128)(2,1)} %reshape.54), calls=%async_computation.1 | async-start | bytes 524288 | tf_op jit(solution)/shard_map/all_to_all | solution.py:130
  42.9 2.8 %fusion.1 = bf16[1,1280,1280]{2,1,0:T(8,128)(2,1)} fusion(bf16[96,2560]{1,0:T(8,128)(2,1)S(1)} %all_gather.3, f32[96,1280]{1,0:T(8,128)S(1)} %fusion.8), kind=kOutput, calls=%fused_computation.3 | convolution fusion | flops 316825600 | bytes 4014080 | tf_op jit(solution)/shard_map/dot_general | solution.py:15
  45.7 7.8 %all-to-all-done.1 = bf16[16,60,128]{2,1,0:T(8,128)(2,1)S(1)} async-done(((bf16[16,60,128]{2,1,0:T(8,128)(2,1)}), bf16[16,60,128]{2,1,0:T(8,128)(2,1)S(1)}, u32[]{:S(2)}, u32[]{:S(2)}) %all-to-all-start.1) | async-done | bytes 245792 | tf_op jit(solution)/shard_map/all_to_all | solution.py:130
  55.0 2.8 %fusion = bf16[1,1280,1280]{2,1,0:T(8,128)(2,1)} fusion(bf16[96,1280]{1,0:T(8,128)(2,1)S(1)} %fusion.18, bf16[96,2560]{1,0:T(8,128)(2,1)S(1)} %all_gather.3), kind=kOutput, calls=%fused_computation.2 | convolution fusion | flops 316211200 | bytes 3768320 | tf_op jit(solution)/shard_map/dot_general | solution.py:15
  57.7 0.7 reshape.56
  58.4 3.5 %all-to-all-start.2 = ((f32[16,15,128]{2,1,0:T(8,128)}), f32[16,15,128]{2,1,0:T(8,128)S(1)}, u32[]{:S(2)}, u32[]{:S(2)}) async-start(f32[16,15,128]{2,1,0:T(8,128)} %reshape.56), calls=%async_computation.2 | async-start | bytes 262144 | tf_op jit(solution)/shard_map/all_to_all | solution.py:91
  62.4 7.8 %all-to-all-done.2 = f32[16,15,128]{2,1,0:T(8,128)S(1)} async-done(((f32[16,15,128]{2,1,0:T(8,128)}), f32[16,15,128]{2,1,0:T(8,128)S(1)}, u32[]{:S(2)}, u32[]{:S(2)}) %all-to-all-start.2) | async-done | bytes 122912 | tf_op jit(solution)/shard_map/all_to_all | solution.py:91
  70.9 3.5 %all-to-all-start.3 = ((f32[16,15,128]{2,1,0:T(8,128)}), f32[16,15,128]{2,1,0:T(8,128)S(1)}, u32[]{:S(2)}, u32[]{:S(2)}) async-start(f32[16,15,128]{2,1,0:T(8,128)} %broadcast_in_dim.20), calls=%async_computation.3 | async-start | bytes 262144 | tf_op jit(solution)/shard_map/all_to_all | solution.py:96
  74.5 1.3 %fusion.14 = bf16[256,1280]{1,0:T(8,128)(2,1)} fusion(f32[256,1280]{1,0:T(8,128)S(1)} %fusion.50, bf16[48,2560]{1,0:T(8,128)(2,1)S(1)} %reshape.55, f32[256,48]{0,1:T(8,128)S(1)} %get-tuple-element.13, f32[48]{0:T(128)S(1)} %get-tuple-element.7, f32[48]{0:T(128)S(1)} %get-tuple-element.9), kind=kOutput, calls=%fused_computation.17 | convolution fusion | flops 32149504 | bytes 2139136 | tf_op jit(solution)/shard_map/dot_general | solution.py:54
  75.7 6.5 %all-to-all-done.3 = f32[16,15,128]{2,1,0:T(8,128)S(1)} async-done(((f32[16,15,128]{2,1,0:T(8,128)}), f32[16,15,128]{2,1,0:T(8,128)S(1)}, u32[]{:S(2)}, u32[]{:S(2)}) %all-to-all-start.3) | async-done | bytes 122912 | tf_op jit(solution)/shard_map/all_to_all | solution.py:96
  82.3 1.3 %convolution_convert_fusion.2 = bf16[256,1280]{1,0:T(8,128)(2,1)} fusion(bf16[48,2560]{1,0:T(8,128)(2,1)S(1)} %reshape.55, f32[256,48]{0,1:T(8,128)S(1)} %get-tuple-element.13, f32[256]{0:T(256)S(1)} %get-tuple-element.8, f32[256]{0:T(256)S(1)} %get-tuple-element.10, pred[48]{0:T(512)(128)(4,1)S(1)} %lt.35), kind=kOutput, calls=%fused_computation.18 | convolution fusion | flops 31834112 | bytes 829952 | tf_op jit(solution)/shard_map/dot_general | solution.py:133
  83.7 0.7 maximum_bitcast_fusion
  (40 shorter events, 5.5 us)
Async XLA Ops:
  0.6 1.1 %copy-start = (bf16[256,1280]{1,0:T(8,128)(2,1)S(1)}, bf16[256,1280]{1,0:T(8,128)(2,1)}, u32[]{:S(2)}) copy-start(bf16[256,1280]{1,0:T(8,128)(2,1)} %param.6) | copy-start | bytes 1966084
  6.0 18.2 %all-to-all-start = ((bf16[16,60,128]{2,1,0:T(8,128)(2,1)}), bf16[16,60,128]{2,1,0:T(8,128)(2,1)S(1)}, u32[]{:S(2)}, u32[]{:S(2)}) async-start(bf16[16,60,128]{2,1,0:T(8,128)(2,1)} %reshape.52), calls=%async_computation | async-start | bytes 524288 | tf_op jit(solution)/shard_map/all_to_all | solution.py:111
  26.7 9.3 %slice-start = ((s8[6553600]{0:T(1024)(128)(4,1)}), s8[4194304]{0:T(1024)(128)(4,1)S(1)}, s32[]{:S(2)}) async-start(s8[6553600]{0:T(1024)(128)(4,1)} %bitcast.34), calls=%async_computation.4 | async-start | bytes 8388608
  29.9 6.1 %slice-start.1 = ((s8[6553600]{0:T(1024)(128)(4,1)}), s8[2359296]{0:T(1024)(128)(4,1)S(1)}, s32[]{:S(2)}) async-start(s8[6553600]{0:T(1024)(128)(4,1)} %bitcast.34), calls=%async_computation.5 | async-start | bytes 4718592
  35.8 1.6 %collective-permute-start = (f32[48,1280]{1,0:T(8,128)S(1)}, f32[48,1280]{1,0:T(8,128)S(1)}, u32[]{:S(2)}, u32[]{:S(2)}) collective-permute-start(f32[48,1280]{1,0:T(8,128)S(1)} %constant_dynamic-slice_fusion.2), channel_id=1, source_target_pairs={{0,16},{16,0},{1,17},{17,1},{2,18},{18,2},{3,19},{19,3},{4,20},{20... | collective-permute-start | bytes 737288 | tf_op jit(solution)/shard_map/ppermute | solution.py:81
  36.7 1.6 %collective-permute-start.1 = (f32[48,1280]{1,0:T(8,128)S(1)}, f32[48,1280]{1,0:T(8,128)S(1)}, u32[]{:S(2)}, u32[]{:S(2)}) collective-permute-start(f32[48,1280]{1,0:T(8,128)S(1)} %constant_dynamic-slice_fusion.1), channel_id=1, source_target_pairs={{0,16},{16,0},{1,17},{17,1},{2,18},{18,2},{3,19},{19,3},{4,20},{20... | collective-permute-start | bytes 737288 | tf_op jit(solution)/shard_map/ppermute | solution.py:81
  38.3 15.8 %copy-start.1 = (bf16[256,1280]{1,0:T(8,128)(2,1)S(1)}, bf16[256,1280]{1,0:T(8,128)(2,1)}, u32[]{:S(2)}) copy-start(bf16[256,1280]{1,0:T(8,128)(2,1)} %param.11) | copy-start | bytes 1966084
  39.4 14.2 %all-to-all-start.1 = ((bf16[16,60,128]{2,1,0:T(8,128)(2,1)}), bf16[16,60,128]{2,1,0:T(8,128)(2,1)S(1)}, u32[]{:S(2)}, u32[]{:S(2)}) async-start(bf16[16,60,128]{2,1,0:T(8,128)(2,1)} %reshape.54), calls=%async_computation.1 | async-start | bytes 524288 | tf_op jit(solution)/shard_map/all_to_all | solution.py:130
  54.2 7.8 %copy-start.2 = (bf16[1280,48]{0,1:T(8,128)(2,1)S(1)}, bf16[1280,48]{0,1:T(8,128)(2,1)}, u32[]{:S(2)}) copy-start(bf16[1280,48]{0,1:T(8,128)(2,1)} %param.7) | copy-start | bytes 368644
  54.9 2.8 %collective-permute-start.2 = (f32[48,640]{1,0:T(8,128)S(1)}, f32[48,640]{1,0:T(8,128)S(1)}, u32[]{:S(2)}, u32[]{:S(2)}) collective-permute-start(f32[48,640]{1,0:T(8,128)S(1)} %constant_dynamic-slice_fusion), channel_id=1, source_target_pairs={{0,16},{16,0},{1,17},{17,1},{2,18},{18,2},{3,19},{19,3},{4,20},{20... | collective-permute-start | bytes 368648 | tf_op jit(solution)/shard_map/ppermute | solution.py:90
  58.4 11.8 %all-to-all-start.2 = ((f32[16,15,128]{2,1,0:T(8,128)}), f32[16,15,128]{2,1,0:T(8,128)S(1)}, u32[]{:S(2)}, u32[]{:S(2)}) async-start(f32[16,15,128]{2,1,0:T(8,128)} %reshape.56), calls=%async_computation.2 | async-start | bytes 262144 | tf_op jit(solution)/shard_map/all_to_all | solution.py:91
  70.9 11.3 %all-to-all-start.3 = ((f32[16,15,128]{2,1,0:T(8,128)}), f32[16,15,128]{2,1,0:T(8,128)S(1)}, u32[]{:S(2)}, u32[]{:S(2)}) async-start(f32[16,15,128]{2,1,0:T(8,128)} %broadcast_in_dim.20), calls=%async_computation.3 | async-start | bytes 262144 | tf_op jit(solution)/shard_map/all_to_all | solution.py:96
  82.3 1.4 %collective-permute-start.3 = (f32[48,640]{1,0:T(8,128)S(1)}, f32[48,640]{1,0:T(8,128)S(1)}, u32[]{:S(2)}, u32[]{:S(2)}) collective-permute-start(f32[48,640]{1,0:T(8,128)S(1)} %reshape.57), channel_id=1, source_target_pairs={{0,16},{16,0},{1,17},{17,1},{2,18},{18,2},{3,19},{19,3},{4,20},{20... | collective-permute-start | bytes 368648 | tf_op jit(solution)/shard_map/ppermute | solution.py:98

commit v2 on v1

--- a/solution.py
+++ b/solution.py
@@ -75,9 +75,7 @@
 
 def sum_own_half(partial):
     rows = partial.shape[0] // 2
-    mine = lax.axis_index("dp")
-    kept = lax.dynamic_slice_in_dim(partial, mine * rows, rows, 0)
-    given = lax.dynamic_slice_in_dim(partial, (1 - mine) * rows, rows, 0)
+    kept, given = partial[:rows], partial[rows:]
     return kept + lax.ppermute(given, "dp", [(0, 1), (1, 0)])
 
 
@@ -116,7 +114,7 @@
     offset = lax.axis_index("dp") * half_width
     first_half = lax.dynamic_slice_in_dim(first_proj, offset, half_width, 0)
     second_half = lax.dynamic_slice_in_dim(second_proj, offset, half_width, 0)
-    both = lax.all_gather(arrived, "dp", axis=0, tiled=True)
+    both = jnp.concatenate([arrived, lax.ppermute(arrived, "dp", [(0, 1), (1, 0)])], axis=0)
     both_rows, both_grads = both[:, :D], both[:, D:]
     values, hidden, slopes = expert_front(both_rows, first_half, second_half)
     grad_rows, grad_first, grad_second = expert_back(

time: 85 us -> 84.4 us (level)
  blocking collectives: 2.16 us -> 0 us
  waiting for transfers between devices: 33.2 us -> 34.7 us
    all_gather x1 -> x0, blocking collectives: 2.16 us -> none  [local(): both = lax.all_gather(arrived, 'dp', axis=0, tiled=True)]
    ppermute x0 -> x1, waiting for transfers between devices: none -> 1.47 us  [local(): lax.ppermute(arrived, 'dp', [(0, 1), (1, 0)])]
  transfers between devices with their start and end apart: 8 -> 9, of which waited for: 6 -> 6; matrix products, arithmetic and copies ran while one was open for 11% -> 15% of each run, Pallas kernels for 0% -> 0%
where the time goes in v2:
time: 84.4 us; the launch traced here: 83.9 us
  waiting for transfers between devices  34.7 us (41%)
  matrix products  22.2 us (26%)
  starting transfers between devices  19.8 us (23%)
  local copies, waits for them, and re-layouts  4.48 us (5%)
  other arithmetic  1.88 us (2%)
  between operations  0.91 us (1%)
    dot_general x10, matrix products, contract(): lax.dot_general(left, right, (((left_dim,), (right_dim,)), ((), ())), pre...  14.8 us
    all_to_all x1, waiting for transfers between devices, local(): lax.all_to_all(outgoing, 'expert', split_axis=0, concat_axis=0, tiled=True)  9.86 us
    all_to_all x1, starting transfers between devices, local(): lax.all_to_all(outgoing, 'expert', split_axis=0, concat_axis=0, tiled=True)  8.34 us
    all_to_all x1, waiting for transfers between devices, sum_everywhere(): lax.all_to_all(term.reshape(experts, -1, 128), 'expert', split_axis=0, co...  7.85 us
    all_to_all x1, waiting for transfers between devices, local(): lax.all_to_all(returning, 'expert', split_axis=0, concat_axis=0, tiled=True)  7.84 us
    all_to_all x1, waiting for transfers between devices, sum_everywhere(): lax.all_to_all(copies, 'expert', split_axis=0, concat_axis=0, tiled=True)  6.49 us
    all_to_all x1, starting transfers between devices, local(): lax.all_to_all(returning, 'expert', split_axis=0, concat_axis=0, tiled=True)  3.55 us
    all_to_all x1, starting transfers between devices, sum_everywhere(): lax.all_to_all(term.reshape(experts, -1, 128), 'expert', split_axis=0, co...  3.52 us
  transfers between devices with their start and end apart: 9, of which 6 were waited for; matrix products, arithmetic and copies ran while one was open for 15% of the time, Pallas kernels for 0%

profile of v2, /device:TPU:0, one launch (start us, length us, event | category | flops | bytes accessed | tf_op | source)
XLA Modules:
  0.0 83.9 jit_solution(15367330660268940701)
XLA Ops:
  0.6 0.8 iota_compare_fusion
  1.7 1.4 %fusion.53 = (f32[48]{0:T(128)S(1)}, f32[256]{0:T(256)S(1)}, f32[256,48]{0,1:T(8,128)S(1)}) fusion(pred[48]{0:T(512)(128)(4,1)S(1)} %lt.27, bf16[256,1280]{1,0:T(8,128)(2,1)S(1)} %copy-done, bf16[1280,48]{0,1:T(8,128)(2,1)} %param.7), kind=kOutput, calls=%fused_computation.74 | convolution fusion | flops 31493840 | bytes 828656 | tf_op jit(solution)/shard_map/dot_general | solution.py:38
  3.6 1.4 %convolution_convert_fusion.3 = bf16[48,1280]{1,0:T(8,128)(2,1)S(1)} fusion(bf16[256,1280]{1,0:T(8,128)(2,1)} %param.11, f32[256,48]{0,1:T(8,128)S(1)} %get-tuple-element.13, f32[256]{0:T(256)S(1)} %get-tuple-element.8, f32[256]{0:T(256)S(1)} %get-tuple-element.10, pred[48]{0:T(512)(128)(4,1)S(1)} %lt.27), kind=kOutput, calls=%fused_computation.21 | convolution fusion | flops 31567872 | bytes 829488 | tf_op jit(solution)/shard_map/dot_general | solution.py:15
  5.0 1.0 %reshape.52 = bf16[16,60,128]{2,1,0:T(8,128)(2,1)} reshape(bf16[48,2560]{1,0:T(8,128)(2,1)S(1)} %pad_maximum_fusion) | data formatting | bytes 491520 | tf_op jit(solution)/shard_map/reshape | solution.py:108
  6.0 8.3 %all-to-all-start = ((bf16[16,60,128]{2,1,0:T(8,128)(2,1)}), bf16[16,60,128]{2,1,0:T(8,128)(2,1)S(1)}, u32[]{:S(2)}, u32[]{:S(2)}) async-start(bf16[16,60,128]{2,1,0:T(8,128)(2,1)} %reshape.52), calls=%async_computation | async-start | bytes 524288 | tf_op jit(solution)/shard_map/all_to_all | solution.py:109
  14.4 9.9 %all-to-all-done = bf16[16,60,128]{2,1,0:T(8,128)(2,1)S(1)} async-done(((bf16[16,60,128]{2,1,0:T(8,128)(2,1)}), bf16[16,60,128]{2,1,0:T(8,128)(2,1)S(1)}, u32[]{:S(2)}, u32[]{:S(2)}) %all-to-all-start) | async-done | bytes 245792 | tf_op jit(solution)/shard_map/all_to_all | solution.py:109
  24.6 1.5 %collective-permute-done = bf16[48,2560]{1,0:T(8,128)(2,1)S(1)} collective-permute-done((bf16[48,2560]{1,0:T(8,128)(2,1)S(1)}, bf16[48,2560]{1,0:T(8,128)(2,1)S(1)}, u32[]{:S(2)}, u32[]{:S(2)}) %collective-permute-start) | collective-permute-done | bytes 245792 | tf_op jit(solution)/shard_map/ppermute | solution.py:117
  26.1 3.2 %fusion.8 = f32[96,1280]{1,0:T(8,128)S(1)} fusion(bf16[1,2560,1280]{2,1,0:T(8,128)(2,1)} %param.9, s32[]{:T(128)S(6)} %select_n.27, bf16[96,2560]{1,0:T(8,128)(2,1)S(1)} %constant_dynamic-update-slice_fusion), kind=kOutput, calls=%fused_computation.10 | convolution fusion | flops 314572800 | bytes 4014084 | tf_op jit(solution)/shard_map/dot_general | solution.py:15
  29.4 2.7 %fusion.4 = f32[96,1280]{1,0:T(8,128)S(1)} fusion(bf16[1,2560,1280]{2,1,0:T(8,128)(2,1)} %param.10, s32[]{:T(128)S(6)} %select_n.27, f32[96,1280]{1,0:T(8,128)S(1)} %fusion.8), kind=kOutput, calls=%fused_computation.6 | convolution fusion | flops 315187200 | bytes 4259844 | tf_op jit(solution)/shard_map/dot_general | solution.py:64
  32.4 3.1 %fusion.18 = bf16[96,1280]{1,0:T(8,128)(2,1)S(1)} fusion(bf16[1,2560,1280]{2,1,0:T(8,128)(2,1)} %param.10, s32[]{:T(128)S(6)} %select_n.27, f32[96,1280]{1,0:T(8,128)S(1)} %fusion.8, bf16[96,2560]{1,0:T(8,128)(2,1)S(1)} %constant_dynamic-update-slice_fusion), kind=kOutput, calls=%fused_computation.20 | convolution fusion | flops 315801600 | bytes 4259844 | tf_op jit(solution)/shard_map/dot_general | solution.py:15
  36.6 1.1 %collective-permute-done.2 = f32[48,1280]{1,0:T(8,128)S(1)} collective-permute-done((f32[48,1280]{1,0:T(8,128)S(1)}, f32[48,1280]{1,0:T(8,128)S(1)}, u32[]{:S(2)}, u32[]{:S(2)}) %collective-permute-start.2) | collective-permute-done | bytes 245792 | tf_op jit(solution)/shard_map/ppermute | solution.py:79
  37.8 1.0 %reshape.54 = bf16[16,60,128]{2,1,0:T(8,128)(2,1)} reshape(bf16[48,2560]{1,0:T(8,128)(2,1)S(1)} %pad_maximum_fusion.1) | data formatting | bytes 491520 | tf_op jit(solution)/shard_map/reshape | solution.py:127
  38.8 3.5 %all-to-all-start.1 = ((bf16[16,60,128]{2,1,0:T(8,128)(2,1)}), bf16[16,60,128]{2,1,0:T(8,128)(2,1)S(1)}, u32[]{:S(2)}, u32[]{:S(2)}) async-start(bf16[16,60,128]{2,1,0:T(8,128)(2,1)} %reshape.54), calls=%async_computation.1 | async-start | bytes 524288 | tf_op jit(solution)/shard_map/all_to_all | solution.py:128
  42.4 2.8 %fusion.1 = bf16[1,1280,1280]{2,1,0:T(8,128)(2,1)} fusion(bf16[96,2560]{1,0:T(8,128)(2,1)S(1)} %constant_dynamic-update-slice_fusion, f32[96,1280]{1,0:T(8,128)S(1)} %fusion.8), kind=kOutput, calls=%fused_computation.3 | convolution fusion | flops 316825600 | bytes 4014080 | tf_op jit(solution)/shard_map/dot_general | solution.py:15
  45.2 7.8 %all-to-all-done.1 = bf16[16,60,128]{2,1,0:T(8,128)(2,1)S(1)} async-done(((bf16[16,60,128]{2,1,0:T(8,128)(2,1)}), bf16[16,60,128]{2,1,0:T(8,128)(2,1)S(1)}, u32[]{:S(2)}, u32[]{:S(2)}) %all-to-all-start.1) | async-done | bytes 245792 | tf_op jit(solution)/shard_map/all_to_all | solution.py:128
  54.4 2.8 %fusion = bf16[1,1280,1280]{2,1,0:T(8,128)(2,1)} fusion(bf16[96,1280]{1,0:T(8,128)(2,1)S(1)} %fusion.18, bf16[96,2560]{1,0:T(8,128)(2,1)S(1)} %constant_dynamic-update-slice_fusion), kind=kOutput, calls=%fused_computation.2 | convolution fusion | flops 316211200 | bytes 3768320 | tf_op jit(solution)/shard_map/dot_general | solution.py:15
  57.2 0.7 reshape.56
  57.9 3.5 %all-to-all-start.2 = ((f32[16,15,128]{2,1,0:T(8,128)}), f32[16,15,128]{2,1,0:T(8,128)S(1)}, u32[]{:S(2)}, u32[]{:S(2)}) async-start(f32[16,15,128]{2,1,0:T(8,128)} %reshape.56), calls=%async_computation.2 | async-start | bytes 262144 | tf_op jit(solution)/shard_map/all_to_all | solution.py:89
  61.9 7.8 %all-to-all-done.2 = f32[16,15,128]{2,1,0:T(8,128)S(1)} async-done(((f32[16,15,128]{2,1,0:T(8,128)}), f32[16,15,128]{2,1,0:T(8,128)S(1)}, u32[]{:S(2)}, u32[]{:S(2)}) %all-to-all-start.2) | async-done | bytes 122912 | tf_op jit(solution)/shard_map/all_to_all | solution.py:89
  70.4 3.5 %all-to-all-start.3 = ((f32[16,15,128]{2,1,0:T(8,128)}), f32[16,15,128]{2,1,0:T(8,128)S(1)}, u32[]{:S(2)}, u32[]{:S(2)}) async-start(f32[16,15,128]{2,1,0:T(8,128)} %broadcast_in_dim.20), calls=%async_computation.3 | async-start | bytes 262144 | tf_op jit(solution)/shard_map/all_to_all | solution.py:94
  73.9 1.3 %fusion.14 = bf16[256,1280]{1,0:T(8,128)(2,1)} fusion(f32[256,1280]{1,0:T(8,128)S(1)} %fusion.52, bf16[48,2560]{1,0:T(8,128)(2,1)S(1)} %reshape.55, f32[256,48]{0,1:T(8,128)S(1)} %get-tuple-element.13, f32[48]{0:T(128)S(1)} %get-tuple-element.7, f32[48]{0:T(128)S(1)} %get-tuple-element.9), kind=kOutput, calls=%fused_computation.17 | convolution fusion | flops 32149504 | bytes 2139136 | tf_op jit(solution)/shard_map/dot_general | solution.py:54
  75.2 6.5 %all-to-all-done.3 = f32[16,15,128]{2,1,0:T(8,128)S(1)} async-done(((f32[16,15,128]{2,1,0:T(8,128)}), f32[16,15,128]{2,1,0:T(8,128)S(1)}, u32[]{:S(2)}, u32[]{:S(2)}) %all-to-all-start.3) | async-done | bytes 122912 | tf_op jit(solution)/shard_map/all_to_all | solution.py:94
  81.8 1.3 %convolution_convert_fusion.2 = bf16[256,1280]{1,0:T(8,128)(2,1)} fusion(bf16[48,2560]{1,0:T(8,128)(2,1)S(1)} %reshape.55, f32[256,48]{0,1:T(8,128)S(1)} %get-tuple-element.13, f32[256]{0:T(256)S(1)} %get-tuple-element.8, f32[256]{0:T(256)S(1)} %get-tuple-element.10, pred[48]{0:T(512)(128)(4,1)S(1)} %lt.27), kind=kOutput, calls=%fused_computation.18 | convolution fusion | flops 31834112 | bytes 829952 | tf_op jit(solution)/shard_map/dot_general | solution.py:131
  83.2 0.7 maximum_bitcast_fusion
  (43 shorter events, 5.4 us)
Async XLA Ops:
  0.6 1.1 %copy-start = (bf16[256,1280]{1,0:T(8,128)(2,1)S(1)}, bf16[256,1280]{1,0:T(8,128)(2,1)}, u32[]{:S(2)}) copy-start(bf16[256,1280]{1,0:T(8,128)(2,1)} %param.6) | copy-start | bytes 1966084
  6.0 18.2 %all-to-all-start = ((bf16[16,60,128]{2,1,0:T(8,128)(2,1)}), bf16[16,60,128]{2,1,0:T(8,128)(2,1)S(1)}, u32[]{:S(2)}, u32[]{:S(2)}) async-start(bf16[16,60,128]{2,1,0:T(8,128)(2,1)} %reshape.52), calls=%async_computation | async-start | bytes 524288 | tf_op jit(solution)/shard_map/all_to_all | solution.py:109
  24.5 1.6 %collective-permute-start = (bf16[48,2560]{1,0:T(8,128)(2,1)S(1)}, bf16[48,2560]{1,0:T(8,128)(2,1)S(1)}, u32[]{:S(2)}, u32[]{:S(2)}) collective-permute-start(bf16[48,2560]{1,0:T(8,128)(2,1)S(1)} %reshape.53), channel_id=1, source_target_pairs={{0,16},{16,0},{1,17},{17,1},{2,18},{18,2},{3,19},{19,3},{4,20},{20... | collective-permute-start | bytes 737288 | tf_op jit(solution)/shard_map/ppermute | solution.py:117
  26.1 9.3 %slice-start = ((s8[6553600]{0:T(1024)(128)(4,1)}), s8[4194304]{0:T(1024)(128)(4,1)S(1)}, s32[]{:S(2)}) async-start(s8[6553600]{0:T(1024)(128)(4,1)} %bitcast.34), calls=%async_computation.4 | async-start | bytes 8388608
  29.4 6.1 %slice-start.1 = ((s8[6553600]{0:T(1024)(128)(4,1)}), s8[2359296]{0:T(1024)(128)(4,1)S(1)}, s32[]{:S(2)}) async-start(s8[6553600]{0:T(1024)(128)(4,1)} %bitcast.34), calls=%async_computation.5 | async-start | bytes 4718592
  32.2 4.4 %collective-permute-start.1 = (f32[48,1280]{1,0:T(8,128)S(1)}, f32[48,1280]{1,0:T(8,128)S(1)}, u32[]{:S(2)}, u32[]{:S(2)}) collective-permute-start(f32[48,1280]{1,0:T(8,128)S(1)} %slice.34), channel_id=1, source_target_pairs={{0,16},{16,0},{1,17},{17,1},{2,18},{18,2},{3,19},{19,3},{4,20},{20... | collective-permute-start | bytes 737288 | tf_op jit(solution)/shard_map/ppermute | solution.py:79
  36.2 1.6 %collective-permute-start.2 = (f32[48,1280]{1,0:T(8,128)S(1)}, f32[48,1280]{1,0:T(8,128)S(1)}, u32[]{:S(2)}, u32[]{:S(2)}) collective-permute-start(f32[48,1280]{1,0:T(8,128)S(1)} %slice.37), channel_id=1, source_target_pairs={{0,16},{16,0},{1,17},{17,1},{2,18},{18,2},{3,19},{19,3},{4,20},{20... | collective-permute-start | bytes 737288 | tf_op jit(solution)/shard_map/ppermute | solution.py:79
  37.8 15.8 %copy-start.1 = (bf16[256,1280]{1,0:T(8,128)(2,1)S(1)}, bf16[256,1280]{1,0:T(8,128)(2,1)}, u32[]{:S(2)}) copy-start(bf16[256,1280]{1,0:T(8,128)(2,1)} %param.11) | copy-start | bytes 1966084
  38.8 14.2 %all-to-all-start.1 = ((bf16[16,60,128]{2,1,0:T(8,128)(2,1)}), bf16[16,60,128]{2,1,0:T(8,128)(2,1)S(1)}, u32[]{:S(2)}, u32[]{:S(2)}) async-start(bf16[16,60,128]{2,1,0:T(8,128)(2,1)} %reshape.54), calls=%async_computation.1 | async-start | bytes 524288 | tf_op jit(solution)/shard_map/all_to_all | solution.py:128
  53.7 7.8 %copy-start.2 = (bf16[1280,48]{0,1:T(8,128)(2,1)S(1)}, bf16[1280,48]{0,1:T(8,128)(2,1)}, u32[]{:S(2)}) copy-start(bf16[1280,48]{0,1:T(8,128)(2,1)} %param.7) | copy-start | bytes 368644
  54.3 2.8 %collective-permute-start.3 = (f32[48,640]{1,0:T(8,128)S(1)}, f32[48,640]{1,0:T(8,128)S(1)}, u32[]{:S(2)}, u32[]{:S(2)}) collective-permute-start(f32[48,640]{1,0:T(8,128)S(1)} %constant_dynamic-slice_fusion), channel_id=1, source_target_pairs={{0,16},{16,0},{1,17},{17,1},{2,18},{18,2},{3,19},{19,3},{4,20},{20... | collective-permute-start | bytes 368648 | tf_op jit(solution)/shard_map/ppermute | solution.py:88
  57.9 11.8 %all-to-all-start.2 = ((f32[16,15,128]{2,1,0:T(8,128)}), f32[16,15,128]{2,1,0:T(8,128)S(1)}, u32[]{:S(2)}, u32[]{:S(2)}) async-start(f32[16,15,128]{2,1,0:T(8,128)} %reshape.56), calls=%async_computation.2 | async-start | bytes 262144 | tf_op jit(solution)/shard_map/all_to_all | solution.py:89
  70.4 11.3 %all-to-all-start.3 = ((f32[16,15,128]{2,1,0:T(8,128)}), f32[16,15,128]{2,1,0:T(8,128)S(1)}, u32[]{:S(2)}, u32[]{:S(2)}) async-start(f32[16,15,128]{2,1,0:T(8,128)} %broadcast_in_dim.20), calls=%async_computation.3 | async-start | bytes 262144 | tf_op jit(solution)/shard_map/all_to_all | solution.py:94
  81.7 1.4 %collective-permute-start.4 = (f32[48,640]{1,0:T(8,128)S(1)}, f32[48,640]{1,0:T(8,128)S(1)}, u32[]{:S(2)}, u32[]{:S(2)}) collective-permute-start(f32[48,640]{1,0:T(8,128)S(1)} %reshape.57), channel_id=1, source_target_pairs={{0,16},{16,0},{1,17},{17,1},{2,18},{18,2},{3,19},{19,3},{4,20},{20... | collective-permute-start | bytes 368648 | tf_op jit(solution)/shard_map/ppermute | solution.py:96
